TPU v7x, 8 devices: a whole 2x2x1 slice. The times are simulated.
8 devices in a mesh: z: 2 (over z, y), y: 2 (over x), xc: 2 (over core).
Axes of the slice: x: 2, y: 2, z: 1, core: 2. Of those that a mesh axis runs over, the one named last changes fastest.
Arguments:
- tokens_x: bfloat16 [65536, 512], P(('z', 'y', 'xc'))
- grad_y: bfloat16 [65536, 512], P(('z', 'y', 'xc'))
- w_one: bfloat16 [512, 2048], replicated
- w_two: bfloat16 [2048, 512], replicated
- w_three: bfloat16 [512, 2048], replicated
- w_four: bfloat16 [2048, 512], replicated
Outputs:
- output 1: float32 [512, 2048], replicated
- output 2: float32 [2048, 512], replicated
- output 3: float32 [512, 2048], replicated
- output 4: float32 [2048, 512], replicated
All inputs are finite; a program needn't handle non-finite values.
Results may differ from a plain program's by a relative error of at most 0.00328.
Values are sent between devices in bfloat16 or wider.
A program may use at most 1 GiB of HBM per device.

v0:
```python
import functools
import math

import jax
import jax.numpy as jnp
from jax import lax
from jax.experimental import pallas as pl
from jax.experimental.pallas import tpu as pltpu
from jax.sharding import PartitionSpec as P

MESH = pl.DeviceIdType.MESH
GELU_C = math.sqrt(2.0 / math.pi)
GELU_K = 0.044715

N = 8192
D = 512
F = 2048
FB = 256
NB = F // FB
T1 = 512
N1 = N // T1
RH = T1 // 2
T2 = 2048
N2 = N // T2
RC2 = 128
RC1 = 256
KU = 256
RA = 128
UNITS = 2 * (T2 // KU)
TQ = T2 // T1
SLOTS = 4
SEMS = 8
OFFS = {2: (0, 2, 6, 10, 12, 16, 18), 1: (0, 1, 5, 8, 11, 15, 16)}
BASE = {2: 6, 1: 4 * (NB + 2) + 5}
LAST_TRIP = BASE[1] + 4 * (NB - 1) + OFFS[1][-1]

bf16 = jnp.bfloat16
f32 = jnp.float32


def dot(a, b):
    return jnp.dot(a, b, preferred_element_type=f32)


def gelu_half(a):
    sq = a * a
    t = jnp.tanh(a * (GELU_C + (GELU_C * GELU_K) * sq))
    s = 0.5 + 0.5 * t
    return sq, s, a * s


def gelu_and_grad(a):
    sq, s, h = gelu_half(a)
    g = s + (h * (1.0 - s)) * (2.0 * GELU_C + (6.0 * GELU_C * GELU_K) * sq)
    return h, g


def kernel(x_hbm, g_hbm, w1_hbm, w2_hbm, w3_hbm, w4_hbm, out, a1_hbm, da3_hbm,
           gn, gt, hn, ht, w1, w2, w3, w4, w4t, u0, u1, d0, d1, va, vb, xs,
           pacc, rx, sm, r1, r2, rs,
           ld_sem, x_sem, st_sem, ld2_sem, send_sem, recv_sem, loc_sem):
    z = lax.axis_index("z")
    y = lax.axis_index("y")
    c = lax.axis_index("xc")
    partner = (z, y, 1 - c)
    near_a = (lax.rem(z + c, 2), lax.rem(y + 1 - c, 2), c)
    near_b = (lax.rem(z + 1 - c, 2), lax.rem(y + c, 2), c)
    bit_a = y * (1 - c) + z * c
    bit_b = z * (1 - c) + y * c

    barrier = pltpu.get_barrier_semaphore()
    for dev in (partner, near_a, near_b):
        pl.semaphore_signal(barrier, inc=1, device_id=dev, device_id_type=MESH)

    def x_copy(i):
        slot = lax.rem(i, 4)
        return pltpu.make_async_copy(x_hbm.at[pl.ds(i * T1, T1)], xs.at[slot], x_sem.at[slot])

    loads = [
        pltpu.make_async_copy(w1_hbm, w1, ld_sem.at[0]),
        pltpu.make_async_copy(w2_hbm, w2, ld_sem.at[1]),
        pltpu.make_async_copy(g_hbm, gn, ld_sem.at[2]),
        pltpu.make_async_copy(w3_hbm, w3, ld_sem.at[3]),
        pltpu.make_async_copy(w4_hbm, w4, ld_sem.at[4]),
    ]
    loads[0].start()
    x_copy(0).start()
    x_copy(1).start()
    for ld in loads[1:]:
        ld.start()

    hs = (u0, u1)
    ds = (d0, d1)
    vs = (va, vb)

    def a1_store(i, par):
        return pltpu.make_async_copy(vs[par], a1_hbm.at[:, i], st_sem.at[par])

    def h1_tile(par, cc):
        return hs[cc // 4].at[cc % 4] if par == 0 else ds[cc // 4].at[cc % 4]

    def h2_unit(par, m, cc, total):
        term = dot(h1_tile(par, cc)[m * RH:(m + 1) * RH, :], w2[cc * FB:(cc + 1) * FB, :])
        return term if total is None else total + term

    def h2_store(i, m, total, x_rows):
        h2 = (total + x_rows.astype(f32)).astype(bf16)
        hn[pl.ds(pl.multiple_of(i * T1 + m * RH, RH), RH), :] = h2
        ht[i, :, m * RH:(m + 1) * RH] = h2.T

    def fwd_trip(i, par, with_a, with_b, with_gt=True):
        xt = xs.at[lax.rem(i, 4)]
        xp = xs.at[lax.rem(i + 3, 4)]
        total = None
        chunks = NB * (T1 // RA)
        for n in range(chunks):
            if with_a:
                cc, r = n // (T1 // RA), n % (T1 // RA)
                a = dot(xt[r * RA:(r + 1) * RA, :], w1[:, cc * FB:(cc + 1) * FB]).astype(bf16)
                vs[par][cc, r * RA:(r + 1) * RA, :] = a
                _, _, h = gelu_half(a.astype(f32))
                h1_tile(par, cc)[r * RA:(r + 1) * RA, :] = h.astype(bf16)
            if with_b:
                for n2 in range(n * 2 * NB // chunks, (n + 1) * 2 * NB // chunks):
                    m, cc = n2 // NB, n2 % NB
                    total = h2_unit(1 - par, m, cc, total if cc else None)
                    if cc == NB - 1:
                        h2_store(i - 1, m, total, xp[m * RH:(m + 1) * RH, :])
        if with_a and with_gt:
            rows = pl.ds(pl.multiple_of(i * T1, T1), T1)
            gt[i] = gn[rows, :].T

    def fwd_tail_transposes(i):
        lanes = pl.ds(pl.multiple_of(i * (F // N1), F // N1), F // N1)
        w4t[:, lanes] = w4[lanes, :].T

    loads[0].wait()
    x_copy(0).wait()
    x_copy(2).start()
    fwd_trip(0, 0, True, False, False)
    a1_store(0, 0).start()
    for ld in loads[1:]:
        ld.wait()
    gt[0] = gn[:T1, :].T
    fwd_tail_transposes(0)

    def fwd_pair(k, carry):
        for par in (1, 0):
            i = 2 * k + 2 - par

            @pl.when(i >= 2)
            def _():
                a1_store(i - 2, par).wait()

            @pl.when(i + 2 < N1)
            def _():
                x_copy(i + 2).start()

            x_copy(i).wait()
            fwd_trip(i, par, True, True)
            fwd_tail_transposes(i)
            a1_store(i, par).start()
        return carry

    lax.fori_loop(0, N1 // 2 - 1, fwd_pair, 0)
    a1_store(N1 - 3, 1).wait()
    x_copy(N1 - 1).wait()
    fwd_trip(N1 - 1, 1, True, True)
    fwd_tail_transposes(N1 - 1)
    a1_store(N1 - 1, 1).start()
    fwd_trip(N1, 0, False, True)
    for par in (0, 1):
        a1_store(N1 - 2 + par, par).wait()

    pl.semaphore_wait(barrier, 3)

    def half(b):
        return pl.ds(pl.multiple_of(b * (D // 2), D // 2), D // 2)

    def quarter(a, b):
        return pl.ds(pl.multiple_of(a * (D // 2) + b * (D // 4), D // 4), D // 4)

    def remote(src, dst, p, step, dev):
        e = lax.rem(p, SEMS)
        return pltpu.make_async_remote_copy(
            src_ref=src, dst_ref=dst, send_sem=send_sem.at[e, step], recv_sem=recv_sem.at[e, step],
            device_id=dev, device_id_type=MESH)

    def cp_pair(p):
        e = lax.rem(p, 2)
        return remote(pacc.at[e, 1 - c], rx.at[e], p, 0, partner)

    def cp_s1(p):
        e = lax.rem(p, 2)
        return remote(sm.at[e, half(1 - bit_a)], r1.at[e], p, 1, near_a)

    def cp_s2(p):
        e = lax.rem(p, 2)
        return remote(sm.at[e, quarter(bit_a, 1 - bit_b)], r2.at[e], p, 2, near_b)

    def cp_s3(p):
        part = rs.at[lax.rem(p, SLOTS), quarter(bit_a, bit_b)]
        return remote(part, part, p, 3, near_b)

    def cp_s4(p):
        part = rs.at[lax.rem(p, SLOTS), half(bit_a)]
        return remote(part, part, p, 4, near_a)

    def cp_s5(p):
        return remote(rs.at[lax.rem(p, SLOTS)], out.at[p, c], p, 5, partner)

    def cp_loc(p):
        e = lax.rem(p, SLOTS)
        return pltpu.make_async_copy(rs.at[e], out.at[p, c], loc_sem.at[e])

    def h_pair_send(p):
        cp_pair(p).start()

    def h_s1(p):
        cp_pair(p).wait()
        e = lax.rem(p, 2)
        sm[e] = pacc[e, c] + rx[e]
        cp_s1(p).start()

    def h_s2(p):
        cp_s1(p).wait()
        e = lax.rem(p, 2)
        rows = half(bit_a)
        sm[e, rows] = sm[e, rows] + r1[e]
        cp_s2(p).start()

    def h_s3(p):
        cp_s2(p).wait()
        e = lax.rem(p, 2)
        rows = quarter(bit_a, bit_b)
        rs[lax.rem(p, SLOTS), rows] = (sm[e, rows] + r2[e]) * 0.125
        cp_s3(p).start()

    def h_s4(p):
        cp_s3(p).wait()
        cp_s4(p).start()

    def h_s5(p):
        cp_s4(p).wait()
        cp_s5(p).start()
        cp_loc(p).start()

    def h_end(p):
        cp_s5(p).wait()
        cp_loc(p).wait()

    stages = (h_pair_send, h_s1, h_s2, h_s3, h_s4, h_s5, h_end)

    def comm(layer, f, parity):
        for order in (0, 6, 5, 4, 3, 2, 1):
            due = BASE[layer] + OFFS[layer][order]
            if (due - parity) % 2:
                continue
            q = f + (64 - due)
            k = q // 4 - 16

            @pl.when(jnp.logical_and(lax.rem(q, 4) == 0, jnp.logical_and(k >= 0, k < NB)))
            def _():
                stages[order](k if layer == 2 else k + NB)

    def b_unit(lhs0, lhs1, tb, par, rhs, first, u, values):
        half_units = UNITS // 2
        m, kq = u // half_units, u % half_units
        rows = slice(m * (D // 2), (m + 1) * (D // 2))
        lo = kq * KU
        out_values = []
        for idx, lhs in ((0, lhs0), (1, lhs1)):
            value = values[idx] if kq else None
            term = dot(lhs[tb * (T2 // T1) + lo // T1, rows, lo % T1:lo % T1 + KU], rhs[idx][lo // T1, lo % T1:lo % T1 + KU, :])
            value = term if value is None else value + term
            if kq == half_units - 1:
                old = pacc[par, idx, rows, :]
                if first is not None:
                    old = jnp.where(first, 0.0, old)
                pacc[par, idx, rows, :] = old + value
            out_values.append(value)
        return out_values

    def b_some(lhs0, lhs1, tb, par, rhs, first, rc, chunks, values):
        for u in range(rc * UNITS // chunks, (rc + 1) * UNITS // chunks):
            values = b_unit(lhs0, lhs1, tb, par, rhs, first, u, values)
        return values

    def b_part(lhs0, lhs1, tb, par, rhs, between=None):
        values = None
        for u in range(UNITS):
            values = b_unit(lhs0, lhs1, tb, par, rhs, None, u, values)
            if between is not None and u % 2 == 1:
                between(u // 2)

    def da3_store(f, par, e):
        return pltpu.make_async_copy(
            vs[par].at[pl.ds(e * TQ, TQ)], da3_hbm.at[f // N2, pl.ds(lax.rem(f, N2) * TQ, TQ)], st_sem.at[2 * e + par])

    def l2_trip(f, par, e):
        t = lax.rem(f, N2)
        j = f // N2
        col = pl.ds(pl.multiple_of(j * FB, FB), FB)
        before = f + N2 - 1
        tb = lax.rem(before, N2)
        pp = lax.rem(before // N2 + 1, 2)
        w3j = w3[:, col]
        w4j = w4t[:, col]
        rhs = (hs[1 - par], vb.at[pl.ds((1 - e) * TQ, TQ)] if par == 0 else va.at[pl.ds(e * TQ, TQ)])
        values = None
        for rc in range(T2 // RC2):
            rows = pl.ds(pl.multiple_of(t * T2 + rc * RC2, RC2), RC2)
            tile, lo = rc * RC2 // T1, rc * RC2 % T1
            a = dot(hn[rows, :], w3j).astype(bf16).astype(f32)
            d = dot(gn[rows, :], w4j)
            h, g = gelu_and_grad(a)
            hs[par][tile, lo:lo + RC2, :] = h.astype(bf16)
            vs[par][e * TQ + tile, lo:lo + RC2, :] = (d * g).astype(bf16)
            values = b_some(gt, ht, tb, pp, rhs, None if par == 0 else tb == 0, rc, T2 // RC2, values)

    def l2_pair(k, carry):
        e = lax.rem(k, 2)
        comm(2, 2 * k, 0)

        @pl.when(k >= 2)
        def _():
            for par in (0, 1):
                da3_store(2 * k - 4 + par, par, e).wait()

        for par in (0, 1):
            l2_trip(2 * k + par, par, e)
        for par in (0, 1):
            da3_store(2 * k + par, par, e).start()
        return carry

    lax.fori_loop(0, NB * N2 // 2, l2_pair, 0)

    tiles = ((va, vb), ((u0, u1), (d0, d1)))

    def da3_loads(i, e, par):
        tile = tiles[e][par]
        if e == 0:
            return [pltpu.make_async_copy(da3_hbm.at[:, i], tile, ld2_sem.at[par])]
        return [
            pltpu.make_async_copy(da3_hbm.at[pl.ds(h * TQ, TQ), i], tile[h], ld2_sem.at[2 + 2 * par + h])
            for h in (0, 1)]

    def da3_tile(e, par, cc):
        return tiles[0][par].at[cc] if e == 0 else tiles[1][par][cc // 4].at[cc % 4]

    def da3_start(i, e, par):
        for ld in da3_loads(i, e, par):
            ld.start()
        x_copy(i).start()

    def turn_weights(cc):
        cols = slice(cc * FB, (cc + 1) * FB)
        w4[cols, :] = w3[:, cols].T
        w4t[:, cols] = w2[cols, :].T

    for f0 in range(NB * N2 - 4, NB * N2):
        da3_store(f0, f0 % 2, f0 // 2 % 2).wait()
    da3_start(0, 0, 0)
    b_part(gt, ht, N2 - 1, (NB - 1) % 2, (hs[1], vb.at[pl.ds(TQ, TQ)]), turn_weights)
    da3_start(1, 0, 1)
    da3_start(2, 1, 0)
    da3_start(3, 1, 1)

    def dh2_tile(i, e, par):
        for m in (0, 1):
            rows = pl.ds(pl.multiple_of(i * T1 + m * RH, RH), RH)
            total = None
            for cc in range(NB):
                term = dot(da3_tile(e, par, cc)[m * RH:(m + 1) * RH, :], w4[cc * FB:(cc + 1) * FB, :])
                total = term if total is None else total + term
            dh2 = (total + gn[rows, :].astype(f32)).astype(bf16)
            hn[rows, :] = dh2
            ht[i, :, m * RH:(m + 1) * RH] = dh2.T
        gt[i] = xs[lax.rem(i, 4)].T

    def dh2_four(q, carry):
        comm(2, NB * N2 + 2 * q, 0)
        for e in (0, 1):
            for par in (0, 1):
                i = 4 * q + 2 * e + par
                for ld in da3_loads(i, e, par):
                    ld.wait()
                x_copy(i).wait()
            for par in (0, 1):
                dh2_tile(4 * q + 2 * e + par, e, par)

            @pl.when(q < N1 // 4 - 1)
            def _():
                for par in (0, 1):
                    da3_start(4 * q + 4 + 2 * e + par, e, par)
        return carry

    lax.fori_loop(0, N1 // 4, dh2_four, 0)

    base = NB * N2 + N1 // 2

    def a1_load(k, par):
        f = 2 * k + par
        e = lax.rem(k, 2)
        return pltpu.make_async_copy(
            a1_hbm.at[f // N2, pl.ds(lax.rem(f, N2) * TQ, TQ)], vs[par].at[pl.ds(e * TQ, TQ)], x_sem.at[2 * e + par])

    for par in (0, 1):
        a1_load(0, par).start()

    def l1_trip(f, par):
        t = lax.rem(f, N2)
        j = f // N2
        col = pl.ds(pl.multiple_of(j * FB, FB), FB)
        before = f + N2 - 1
        tb = lax.rem(before, N2)
        pp = lax.rem(before // N2 + 1, 2)
        e = lax.rem(f // 2, 2)
        w2j = w4t[:, col]
        rhs = (hs[1 - par], ds[1 - par])
        values = None
        for rc in range(T2 // RC1):
            rows = pl.ds(pl.multiple_of(t * T2 + rc * RC1, RC1), RC1)
            tile, lo = rc * RC1 // T1, rc * RC1 % T1
            a = vs[par][e * TQ + tile, lo:lo + RC1, :].astype(f32)
            d = dot(hn[rows, :], w2j)
            h, g = gelu_and_grad(a)
            hs[par][tile, lo:lo + RC1, :] = h.astype(bf16)
            ds[par][tile, lo:lo + RC1, :] = (d * g).astype(bf16)
            values = b_some(ht, gt, tb, pp, rhs, None if par == 0 else tb == 0, rc, T2 // RC1, values)

    def l1_pair(k, carry):
        for par in (0, 1):
            f = base + 2 * k + par
            comm(2, f, par)
            comm(1, f, par)
            a1_load(k, par).wait()

            @pl.when(2 * k + 2 < NB * N2)
            def _():
                a1_load(k + 1, par).start()

            l1_trip(2 * k + par, par)
        return carry

    lax.fori_loop(0, NB * N2 // 2, l1_pair, 0)
    comm(1, base + NB * N2, 0)
    b_part(ht, gt, N2 - 1, (NB - 1) % 2, (hs[1], ds[1]))

    def tail(k, carry):
        for par in (1, 0):
            comm(1, base + NB * N2 + 2 + 2 * k - par, par)
        return carry

    lax.fori_loop(0, (LAST_TRIP - base - NB * N2 + 1) // 2, tail, 0)


def finish_kernel(sums, o1, o2, o3, o4, buf, flip, in_sem, wide_sem, tall_sem):
    def load(p):
        return pltpu.make_async_copy(sums.at[p], buf.at[p], in_sem.at[p])

    def store_wide(o, j, p):
        return pltpu.make_async_copy(
            buf.at[p, 1], o.at[:, pl.ds(pl.multiple_of(j * FB, FB), FB)], wide_sem.at[p])

    def store_tall(o, j, p):
        return pltpu.make_async_copy(
            flip.at[p], o.at[pl.ds(pl.multiple_of(j * FB, FB), FB), :], tall_sem.at[p])

    for p in range(2 * NB):
        load(p).start()
    for base, wide, tall in ((0, o3, o4), (NB, o1, o2)):
        def step(j, carry):
            p = base + j
            load(p).wait()
            store_wide(wide, j, p).start()
            flip[p] = buf[p, 0].T
            store_tall(tall, j, p).start()
            return carry
        lax.fori_loop(0, NB, step, 0)
    for base, wide, tall in ((0, o3, o4), (NB, o1, o2)):
        def drain(j, carry):
            store_wide(wide, j, base + j).wait()
            store_tall(tall, j, base + j).wait()
            return carry
        lax.fori_loop(0, NB, drain, 0)


def device_step(x_loc, g_loc, w_one, w_two, w_three, w_four):
    any_spec = pl.BlockSpec(memory_space=pl.ANY)
    sums, _, _ = pl.pallas_call(
        kernel,
        name="grads",
        out_shape=(
            jax.ShapeDtypeStruct((2 * NB, 2, D, FB), f32),
            jax.ShapeDtypeStruct((NB, N1, T1, FB), bf16),
            jax.ShapeDtypeStruct((NB, N1, T1, FB), bf16),
        ),
        in_specs=[any_spec] * 6,
        out_specs=(any_spec,) * 3,
        scratch_shapes=[
            pltpu.VMEM((N, D), bf16),
            pltpu.VMEM((N1, D, T1), bf16),
            pltpu.VMEM((N, D), bf16),
            pltpu.VMEM((N1, D, T1), bf16),
            pltpu.VMEM((D, F), bf16),
            pltpu.VMEM((F, D), bf16),
            pltpu.VMEM((D, F), bf16),
            pltpu.VMEM((F, D), bf16),
            pltpu.VMEM((D, F), bf16),
            pltpu.VMEM((TQ, T1, FB), bf16),
            pltpu.VMEM((TQ, T1, FB), bf16),
            pltpu.VMEM((TQ, T1, FB), bf16),
            pltpu.VMEM((TQ, T1, FB), bf16),
            pltpu.VMEM((NB, T1, FB), bf16),
            pltpu.VMEM((NB, T1, FB), bf16),
            pltpu.VMEM((4, T1, D), bf16),
            pltpu.VMEM((2, 2, D, FB), f32),
            pltpu.VMEM((2, D, FB), f32),
            pltpu.VMEM((2, D, FB), f32),
            pltpu.VMEM((2, D // 2, FB), f32),
            pltpu.VMEM((2, D // 4, FB), f32),
            pltpu.VMEM((SLOTS, D, FB), f32),
            pltpu.SemaphoreType.DMA((5,)),
            pltpu.SemaphoreType.DMA((4,)),
            pltpu.SemaphoreType.DMA((4,)),
            pltpu.SemaphoreType.DMA((6,)),
            pltpu.SemaphoreType.DMA((SEMS, 6)),
            pltpu.SemaphoreType.DMA((SEMS, 6)),
            pltpu.SemaphoreType.DMA((SLOTS,)),
        ],
        compiler_params=pltpu.CompilerParams(
            collective_id=0, has_side_effects=True, vmem_limit_bytes=67000000),
        cost_estimate=pl.CostEstimate(flops=20 * N * D * F, bytes_accessed=200 << 20, transcendentals=3 * N * F),
    )(x_loc, g_loc, w_one, w_two, w_three, w_four)
    wide = jax.ShapeDtypeStruct((D, F), f32)
    tall = jax.ShapeDtypeStruct((F, D), f32)
    return pl.pallas_call(
        finish_kernel,
        name="finish",
        out_shape=(wide, tall, wide, tall),
        in_specs=[any_spec],
        out_specs=(any_spec,) * 4,
        scratch_shapes=[
            pltpu.VMEM((2 * NB, 2, D, FB), f32),
            pltpu.VMEM((2 * NB, FB, D), f32),
            pltpu.SemaphoreType.DMA((2 * NB,)),
            pltpu.SemaphoreType.DMA((2 * NB,)),
            pltpu.SemaphoreType.DMA((2 * NB,)),
        ],
        compiler_params=pltpu.CompilerParams(vmem_limit_bytes=40 << 20),
    )(sums)


def solution(mesh):
    batch_spec = P(("z", "y", "xc"), None)
    whole_spec = P(None, None)
    return jax.shard_map(
        device_step,
        mesh=mesh,
        in_specs=(batch_spec, batch_spec, whole_spec, whole_spec, whole_spec, whole_spec),
        out_specs=(whole_spec, whole_spec, whole_spec, whole_spec),
        check_vma=False,
    )
```

profile of v0, /device:TPU:0, one launch (start us, length us, event | category | flops | bytes accessed | tf_op | source)
XLA Modules:
  0.0 267.6 jit_solution(14943693067801388891)
XLA Ops:
  0.6 254.6 %grads.1 = (f32[16,2,512,256]{3,2,1,0:T(8,128)}, bf16[8,16,512,256]{3,2,1,0:T(8,128)(2,1)}, bf16[8,16,512,256]{3,2,1,0:T(8,128)(2,1)}) custom-call(bf16[8192,512]{1,0:T(8,128)(2,1)} %x_hbm.1, bf16[8192,512]{1,0:T(8,128)(2,1)} %g_hbm.1, bf16[512,2048]{1,0:T(8,128)(2,1)} %w1_hbm.1, bf16[2048,512]{1,0:T(8,128)(2,1)} %w2_hbm.1, bf16[512,2048]{1,0:T(8,128)(2,1)} %w3_hbm.1, ...), custom_call_target="tpu_custom_call" | custom-call | flops 171798691840 | bytes 209715200 | tf_op jit(solution)/shard_map/grads/pallas_call | solution.py:491
  255.2 12.1 %finish.1 = (f32[512,2048]{1,0:T(8,128)}, f32[2048,512]{1,0:T(8,128)}, f32[512,2048]{1,0:T(8,128)}, f32[2048,512]{1,0:T(8,128)}) custom-call(f32[16,2,512,256]{3,2,1,0:T(8,128)} %get-tuple-element.5.sums), custom_call_target="tpu_custom_call" | custom-call | tf_op jit(solution)/shard_map/finish/pallas_call | solution.py:538
where the time goes:
time: 268 us
  Pallas kernels  267 us (100%)
    pallas_call x1, Pallas kernels, device_step(): pl.pallas_call(kernel, name='grads', out_shape=(jax.ShapeDtypeStruct((2 *...  255 us
    pallas_call x1, Pallas kernels, device_step(): pl.pallas_call(finish_kernel, name='finish', out_shape=(wide, tall, wide,...  12.1 us

commit v1 on v0

--- a/solution.py
+++ b/solution.py
@@ -24,9 +24,9 @@
 N2 = N // T2
 RC2 = 128
 RC1 = 256
-KU = 256
+KU2 = 512
+KU1 = 256
 RA = 128
-UNITS = 2 * (T2 // KU)
 TQ = T2 // T1
 SLOTS = 4
 SEMS = 8
@@ -168,9 +168,6 @@
     fwd_trip(N1 - 1, 1, True, True)
     fwd_tail_transposes(N1 - 1)
     a1_store(N1 - 1, 1).start()
-    fwd_trip(N1, 0, False, True)
-    for par in (0, 1):
-        a1_store(N1 - 2 + par, par).wait()
 
     pl.semaphore_wait(barrier, 3)
 
@@ -263,15 +260,15 @@
             def _():
                 stages[order](k if layer == 2 else k + NB)
 
-    def b_unit(lhs0, lhs1, tb, par, rhs, first, u, values):
-        half_units = UNITS // 2
+    def b_unit(lhs0, lhs1, tb, par, rhs, first, ku, u, values):
+        half_units = T2 // ku
         m, kq = u // half_units, u % half_units
         rows = slice(m * (D // 2), (m + 1) * (D // 2))
-        lo = kq * KU
+        lo = kq * ku
         out_values = []
         for idx, lhs in ((0, lhs0), (1, lhs1)):
             value = values[idx] if kq else None
-            term = dot(lhs[tb * (T2 // T1) + lo // T1, rows, lo % T1:lo % T1 + KU], rhs[idx][lo // T1, lo % T1:lo % T1 + KU, :])
+            term = dot(lhs[tb * (T2 // T1) + lo // T1, rows, lo % T1:lo % T1 + ku], rhs[idx][lo // T1, lo % T1:lo % T1 + ku, :])
             value = term if value is None else value + term
             if kq == half_units - 1:
                 old = pacc[par, idx, rows, :]
@@ -281,15 +278,16 @@
             out_values.append(value)
         return out_values
 
-    def b_some(lhs0, lhs1, tb, par, rhs, first, rc, chunks, values):
-        for u in range(rc * UNITS // chunks, (rc + 1) * UNITS // chunks):
-            values = b_unit(lhs0, lhs1, tb, par, rhs, first, u, values)
+    def b_some(lhs0, lhs1, tb, par, rhs, first, ku, rc, chunks, values):
+        units = 2 * (T2 // ku)
+        for u in range(rc * units // chunks, (rc + 1) * units // chunks):
+            values = b_unit(lhs0, lhs1, tb, par, rhs, first, ku, u, values)
         return values
 
     def b_part(lhs0, lhs1, tb, par, rhs, between=None):
         values = None
-        for u in range(UNITS):
-            values = b_unit(lhs0, lhs1, tb, par, rhs, None, u, values)
+        for u in range(2 * (T2 // KU1)):
+            values = b_unit(lhs0, lhs1, tb, par, rhs, None, KU1, u, values)
             if between is not None and u % 2 == 1:
                 between(u // 2)
 
@@ -297,7 +295,7 @@
         return pltpu.make_async_copy(
             vs[par].at[pl.ds(e * TQ, TQ)], da3_hbm.at[f // N2, pl.ds(lax.rem(f, N2) * TQ, TQ)], st_sem.at[2 * e + par])
 
-    def l2_trip(f, par, e):
+    def l2_trip(f, par, e, with_b=True):
         t = lax.rem(f, N2)
         j = f // N2
         col = pl.ds(pl.multiple_of(j * FB, FB), FB)
@@ -308,6 +306,7 @@
         w4j = w4t[:, col]
         rhs = (hs[1 - par], vb.at[pl.ds((1 - e) * TQ, TQ)] if par == 0 else va.at[pl.ds(e * TQ, TQ)])
         values = None
+        first = None if par == 0 else tb == 0
         for rc in range(T2 // RC2):
             rows = pl.ds(pl.multiple_of(t * T2 + rc * RC2, RC2), RC2)
             tile, lo = rc * RC2 // T1, rc * RC2 % T1
@@ -316,7 +315,25 @@
             h, g = gelu_and_grad(a)
             hs[par][tile, lo:lo + RC2, :] = h.astype(bf16)
             vs[par][e * TQ + tile, lo:lo + RC2, :] = (d * g).astype(bf16)
-            values = b_some(gt, ht, tb, pp, rhs, None if par == 0 else tb == 0, rc, T2 // RC2, values)
+            if with_b:
+                values = b_some(gt, ht, tb, pp, rhs, first, KU2, rc, T2 // RC2, values)
+            else:
+                values = last_h2(rc, values)
+
+    def last_h2(rc, total):
+        for n2 in range(rc * 2 * NB // (T2 // RC2), (rc + 1) * 2 * NB // (T2 // RC2)):
+            m, cc = n2 // NB, n2 % NB
+            total = h2_unit(1, m, cc, total if cc else None)
+            if cc == NB - 1:
+                h2_store(N1 - 1, m, total, xs[(N1 - 1) % 4, m * RH:(m + 1) * RH, :])
+        return total
+
+    for par in (0, 1):
+        a1_store(N1 - 2 + par, par).wait()
+    l2_trip(0, 0, 0, with_b=False)
+    l2_trip(1, 1, 0)
+    for par in (0, 1):
+        da3_store(par, par, 0).start()
 
     def l2_pair(k, carry):
         e = lax.rem(k, 2)
@@ -333,7 +350,7 @@
             da3_store(2 * k + par, par, e).start()
         return carry
 
-    lax.fori_loop(0, NB * N2 // 2, l2_pair, 0)
+    lax.fori_loop(1, NB * N2 // 2, l2_pair, 0)
 
     tiles = ((va, vb), ((u0, u1), (d0, d1)))
 
@@ -427,7 +444,7 @@
             h, g = gelu_and_grad(a)
             hs[par][tile, lo:lo + RC1, :] = h.astype(bf16)
             ds[par][tile, lo:lo + RC1, :] = (d * g).astype(bf16)
-            values = b_some(ht, gt, tb, pp, rhs, None if par == 0 else tb == 0, rc, T2 // RC1, values)
+            values = b_some(ht, gt, tb, pp, rhs, None if par == 0 else tb == 0, KU1, rc, T2 // RC1, values)
 
     def l1_pair(k, carry):
         for par in (0, 1):

time: 268 us -> 267 us (level)
  no operation moved by 1% of the time
where the time goes in v1:
time: 267 us; the launch traced here: 266 us
  Pallas kernels  266 us (100%)
    pallas_call x1, Pallas kernels, device_step(): pl.pallas_call(kernel, name='grads', out_shape=(jax.ShapeDtypeStruct((2 *...  253 us
    pallas_call x1, Pallas kernels, device_step(): pl.pallas_call(finish_kernel, name='finish', out_shape=(wide, tall, wide,...  12.1 us

profile of v1, /device:TPU:0, one launch (start us, length us, event | category | flops | bytes accessed | tf_op | source)
XLA Modules:
  0.0 266.4 jit_solution(667631436352560043)
XLA Ops:
  0.6 253.4 %grads.1 = (f32[16,2,512,256]{3,2,1,0:T(8,128)}, bf16[8,16,512,256]{3,2,1,0:T(8,128)(2,1)}, bf16[8,16,512,256]{3,2,1,0:T(8,128)(2,1)}) custom-call(bf16[8192,512]{1,0:T(8,128)(2,1)} %x_hbm.1, bf16[8192,512]{1,0:T(8,128)(2,1)} %g_hbm.1, bf16[512,2048]{1,0:T(8,128)(2,1)} %w1_hbm.1, bf16[2048,512]{1,0:T(8,128)(2,1)} %w2_hbm.1, bf16[512,2048]{1,0:T(8,128)(2,1)} %w3_hbm.1, ...), custom_call_target="tpu_custom_call" | custom-call | flops 171798691840 | bytes 209715200 | tf_op jit(solution)/shard_map/grads/pallas_call | solution.py:508
  254.1 12.1 %finish.1 = (f32[512,2048]{1,0:T(8,128)}, f32[2048,512]{1,0:T(8,128)}, f32[512,2048]{1,0:T(8,128)}, f32[2048,512]{1,0:T(8,128)}) custom-call(f32[16,2,512,256]{3,2,1,0:T(8,128)} %get-tuple-element.5.sums), custom_call_target="tpu_custom_call" | custom-call | tf_op jit(solution)/shard_map/finish/pallas_call | solution.py:555

commit v2 on v1

--- a/solution.py
+++ b/solution.py
@@ -76,18 +76,17 @@
         slot = lax.rem(i, 4)
         return pltpu.make_async_copy(x_hbm.at[pl.ds(i * T1, T1)], xs.at[slot], x_sem.at[slot])
 
+    g_head, g_rest = pl.ds(0, N // 2), pl.ds(N // 2, N // 2)
     loads = [
         pltpu.make_async_copy(w1_hbm, w1, ld_sem.at[0]),
         pltpu.make_async_copy(w2_hbm, w2, ld_sem.at[1]),
-        pltpu.make_async_copy(g_hbm, gn, ld_sem.at[2]),
-        pltpu.make_async_copy(w3_hbm, w3, ld_sem.at[3]),
-        pltpu.make_async_copy(w4_hbm, w4, ld_sem.at[4]),
+        pltpu.make_async_copy(g_hbm.at[g_head], gn.at[g_head], ld_sem.at[2]),
+        pltpu.make_async_copy(w4_hbm, w4, ld_sem.at[3]),
+        pltpu.make_async_copy(g_hbm.at[g_rest], gn.at[g_rest], ld_sem.at[4]),
+        pltpu.make_async_copy(w3_hbm, w3, ld_sem.at[5]),
     ]
     loads[0].start()
     x_copy(0).start()
-    x_copy(1).start()
-    for ld in loads[1:]:
-        ld.start()
 
     hs = (u0, u1)
     ds = (d0, d1)
@@ -136,15 +135,23 @@
 
     loads[0].wait()
     x_copy(0).wait()
+    x_copy(1).start()
+    for ld in loads[1:]:
+        ld.start()
     x_copy(2).start()
     fwd_trip(0, 0, True, False, False)
     a1_store(0, 0).start()
-    for ld in loads[1:]:
+    for ld in loads[1:4]:
         ld.wait()
     gt[0] = gn[:T1, :].T
     fwd_tail_transposes(0)
 
     def fwd_pair(k, carry):
+        @pl.when(k == 2)
+        def _():
+            for ld in loads[4:]:
+                ld.wait()
+
         for par in (1, 0):
             i = 2 * k + 2 - par
 
@@ -538,7 +545,7 @@
             pltpu.VMEM((2, D // 2, FB), f32),
             pltpu.VMEM((2, D // 4, FB), f32),
             pltpu.VMEM((SLOTS, D, FB), f32),
-            pltpu.SemaphoreType.DMA((5,)),
+            pltpu.SemaphoreType.DMA((6,)),
             pltpu.SemaphoreType.DMA((4,)),
             pltpu.SemaphoreType.DMA((4,)),
             pltpu.SemaphoreType.DMA((6,)),

time: 267 us -> 266 us (level)
  no operation moved by 1% of the time
where the time goes in v2:
time: 266 us
  Pallas kernels  265 us (100%)
    pallas_call x1, Pallas kernels, device_step(): pl.pallas_call(kernel, name='grads', out_shape=(jax.ShapeDtypeStruct((2 *...  253 us
    pallas_call x1, Pallas kernels, device_step(): pl.pallas_call(finish_kernel, name='finish', out_shape=(wide, tall, wide,...  12.1 us

profile of v2, /device:TPU:0, one launch (start us, length us, event | category | flops | bytes accessed | tf_op | source)
XLA Modules:
  0.0 265.6 jit_solution(14472181057376530778)
XLA Ops:
  0.6 252.7 %grads.1 = (f32[16,2,512,256]{3,2,1,0:T(8,128)}, bf16[8,16,512,256]{3,2,1,0:T(8,128)(2,1)}, bf16[8,16,512,256]{3,2,1,0:T(8,128)(2,1)}) custom-call(bf16[8192,512]{1,0:T(8,128)(2,1)} %x_hbm.1, bf16[8192,512]{1,0:T(8,128)(2,1)} %g_hbm.1, bf16[512,2048]{1,0:T(8,128)(2,1)} %w1_hbm.1, bf16[2048,512]{1,0:T(8,128)(2,1)} %w2_hbm.1, bf16[512,2048]{1,0:T(8,128)(2,1)} %w3_hbm.1, ...), custom_call_target="tpu_custom_call" | custom-call | flops 171798691840 | bytes 209715200 | tf_op jit(solution)/shard_map/grads/pallas_call | solution.py:515
  253.3 12.1 %finish.1 = (f32[512,2048]{1,0:T(8,128)}, f32[2048,512]{1,0:T(8,128)}, f32[512,2048]{1,0:T(8,128)}, f32[2048,512]{1,0:T(8,128)}) custom-call(f32[16,2,512,256]{3,2,1,0:T(8,128)} %get-tuple-element.5.sums), custom_call_target="tpu_custom_call" | custom-call | tf_op jit(solution)/shard_map/finish/pallas_call | solution.py:562
